TPU v7x, 128 devices: a whole 4x4x4 slice. The times are simulated.
128 devices in a mesh: dp: 16 (over x, y), mp: 8 (over z, core).
Axes of the slice: x: 4, y: 4, z: 4, core: 2. Of those that a mesh axis runs over, the one named last changes fastest.
Arguments:
- patches: bfloat16 [768, 64, 1024], P(('dp', 'mp')), may hold values from -6 to 6
- gain_first: float32 [1024], replicated, may hold values from 0.1 to 1.9
- joint_weight: bfloat16 [1024, 3, 1024], P('dp', None, 'mp'), may hold values from -0.1875 to 0.1875
- head_scale: float32 [16], P('mp'), may hold values from 2 to 32
- output_weight: bfloat16 [1024, 1024], P('mp', 'dp'), may hold values from -0.1875 to 0.1875
- gain_second: float32 [1024], replicated, may hold values from 0.3 to 3
- up_weight: bfloat16 [1024, 4096], P('dp', 'mp'), may hold values from -0.1875 to 0.1875
- down_weight: bfloat16 [4096, 1024], P('mp', 'dp'), may hold values from -0.09375 to 0.09375
- gain_final: float32 [1024], replicated, may hold values from 0.1 to 1.9
- project_weight: bfloat16 [1024, 768], replicated, may hold values from -0.1875 to 0.1875
- text_bank: bfloat16 [12288, 768], P(('dp', 'mp')), may hold values from -20000 to 20000
- captions: int32 [768], replicated, may hold values from 0 to 12287
- reference_loss: float32 [768], P(('dp', 'mp')), may hold values from 2 to 20
Outputs:
- learnability: float32 [768], P(('dp', 'mp'))
All inputs are finite; a program needn't handle non-finite values.
Results may differ from a plain program's by a relative error of at most 0.018.
Values may be sent and summed in bfloat16 or wider, within the bound.
No kernel may reach another device: no remote copies, remote signals or barrier semaphores. Data moves between devices by JAX's collectives and lax.ppermute only.
A program may use at most 128 MiB of HBM per device.

v0:
```python
import jax
import jax.numpy as jnp
from jax import lax
from jax.sharding import PartitionSpec as P


def gather_turned(arrays, axis, dims):
    turned = [jnp.moveaxis(a, dim, 0) for a, dim in zip(arrays, dims)]
    both = jnp.concatenate([t.reshape(len(t), -1) for t in turned], axis=1)
    result, at, outs = (lax.all_gather(both, axis, axis=0, tiled=True), 0, [])
    for t, dim in zip(turned, dims):
        slab = result[:, at : at + t[0].size].reshape(-1, *t.shape[1:])
        outs.append(jnp.moveaxis(slab, 0, dim))
        at += t[0].size
    return tuple(outs)


def joined_along(parts, dim):
    lengths = list(parts.shape[1:])
    lengths[dim] *= parts.shape[0]
    return jnp.moveaxis(parts, 0, dim).reshape(lengths)


def sent_to_all(array, axis):
    devices = lax.axis_size(axis)
    return lax.all_to_all(
        jnp.broadcast_to(array[None], (devices, *array.shape)), axis, 0, 0, tiled=True
    )


def gathered_copies(array, axis, dim):
    return joined_along(sent_to_all(array, axis), dim)


def layer_norm(values, gain):
    centre = values - jnp.mean(values, axis=-1, keepdims=True)
    spread = jnp.mean(centre * centre, axis=-1, keepdims=True)
    return centre * lax.rsqrt(spread + 1e-06) * gain


def unit_rows(values):
    return values * lax.rsqrt(jnp.sum(values * values, axis=-1, keepdims=True) + 1e-06)


def attend(normed_rows, joint_full, scales, image_count, patch_count):
    features = normed_rows.shape[1]
    local_heads = scales.shape[0]
    head_width = joint_full.shape[2] // local_heads
    joint = jnp.dot(
        normed_rows, joint_full.reshape(features, -1), preferred_element_type=jnp.float32
    )
    joint = joint.reshape(image_count, patch_count, 3, local_heads, head_width)
    queries = unit_rows(joint[:, :, 0]).astype(jnp.bfloat16)
    key_rows = unit_rows(joint[:, :, 1]).astype(jnp.bfloat16)
    value_rows = joint[:, :, 2].astype(jnp.bfloat16)
    scores = jnp.einsum("bqhd,bkhd->bhqk", queries, key_rows, preferred_element_type=jnp.float32)
    exponent = jnp.exp(scores * scales[None, :, None, None])
    attention = (exponent / jnp.sum(exponent, axis=-1, keepdims=True)).astype(jnp.bfloat16)
    head_out = jnp.einsum(
        "bhqk,bkhd->bqhd", attention, value_rows, preferred_element_type=jnp.float32
    ).astype(jnp.bfloat16)
    return head_out.reshape(image_count * patch_count, local_heads * head_width)


def grouped_local(left_rows, right_cols, groups):
    rows = left_rows.shape[0]
    group_width = left_rows.shape[1] // groups
    left_groups = left_rows.reshape(rows, groups, group_width)
    right_groups = right_cols.reshape(groups, group_width, right_cols.shape[1])
    partial_value = jnp.einsum(
        "rgk,gkn->rgn", left_groups, right_groups, preferred_element_type=jnp.float32
    )
    rounded = lax.optimization_barrier(partial_value.astype(jnp.bfloat16))
    return jnp.sum(rounded.astype(jnp.float32), axis=1)


def shards(
    patches,
    gain_first,
    joint_weight,
    head_scale,
    output_weight,
    gain_second,
    up_weight,
    down_weight,
    gain_final,
    project_weight,
    text_bank,
    captions,
    reference_loss,
):
    joint_full, output_full, up_full, down_full = gather_turned(
        (joint_weight, output_weight, up_weight, down_weight), "dp", (0, 1, 0, 1)
    )
    own_images, patch_count, features = patches.shape
    residual = patches.astype(jnp.float32)
    normed_first = layer_norm(residual, gain_first).astype(jnp.bfloat16)
    groups = lax.axis_size("mp")
    joint_all, output_all, up_all, down_all = (
        lax.all_gather(joint_full, "mp", axis=2, tiled=True),
        lax.all_gather(output_full, "mp", axis=0, tiled=True),
        lax.all_gather(up_full, "mp", axis=1, tiled=True),
        lax.all_gather(down_full, "mp", axis=0, tiled=True),
    )
    scales_all = gathered_copies(head_scale, "mp", 0)
    flat_rows = normed_first.reshape(own_images * patch_count, features)
    head_out = attend(flat_rows, joint_all, scales_all, own_images, patch_count)
    residual_flat = residual.reshape(own_images * patch_count, features)
    residual_two = residual_flat + grouped_local(head_out, output_all, groups)
    normed_second = layer_norm(residual_two, gain_second).astype(jnp.bfloat16)
    upper = jnp.dot(normed_second, up_all, preferred_element_type=jnp.float32)
    hidden = jax.nn.gelu(upper, approximate=False).astype(jnp.bfloat16)
    feed = grouped_local(hidden, down_all, groups)
    pooled = (
        jnp.sum((residual_two + feed).reshape(own_images, patch_count, features), axis=1)
        / patch_count
    )
    pooled_norm = layer_norm(pooled, gain_final).astype(jnp.bfloat16)
    embedded = jnp.dot(pooled_norm, project_weight, preferred_element_type=jnp.float32)
    image_units = unit_rows(embedded).astype(jnp.bfloat16)
    first_row = lax.axis_index(("dp", "mp")) * own_images
    own_captions = lax.dynamic_slice_in_dim(captions, first_row, own_images)
    highest = jnp.full((own_images,), -1e30, jnp.float32)
    logits = lax.dot_general(
        image_units,
        lax.all_gather(text_bank, ("dp", "mp"), axis=0, tiled=True),
        (((1,), (1,)), ((), ())),
        preferred_element_type=jnp.float32,
    )
    new_highest = jnp.maximum(highest, jnp.max(logits, axis=1))
    totals = jnp.sum(jnp.exp(logits - new_highest[:, None]), axis=1)
    text_ids = lax.broadcasted_iota(jnp.int32, logits.shape, 1)
    matched = jnp.sum(jnp.where(text_ids == own_captions[:, None], logits, 0.0), axis=1)
    highest, totals, matched = (new_highest, totals, matched)
    return highest + jnp.log(totals) - matched - reference_loss


def solution(mesh):
    placed = (
        P(("dp", "mp"), None, None),
        P(),
        P("dp", None, "mp"),
        P("mp"),
        P("mp", "dp"),
        P(),
        P("dp", "mp"),
        P("mp", "dp"),
        P(),
        P(),
        P(("dp", "mp"), None),
        P(),
        P(("dp", "mp")),
    )
    return jax.shard_map(
        shards, mesh=mesh, in_specs=placed, out_specs=P(("dp", "mp")), check_vma=False
    )
```

profile of v0, /device:TPU:1, one launch (start us, length us, event | category | flops | bytes accessed | tf_op | source)
XLA Modules:
  0.0 336.5 jit_solution(14013959427415211761)
XLA Ops:
  6.5 0.0 copy-start
  6.5 0.9 copy_bitcast_fusion
  7.5 1.6 pad_maximum_fusion
  9.0 0.0 all-gather.7.cloned.1.call-update
  9.1 0.0 all-gather.11.cloned.1.call-start
  9.1 50.7 %all-gather.7.cloned.1.call-done = bf16[1024,1536]{1,0:T(8,128)(2,1)} async-done(((bf16[64,1536]{1,0:T(8,128)(2,1)}), bf16[1024,1536]{1,0:T(8,128)(2,1)}) %all-gather.7.cloned.1.call-update) | async-done | bytes 3145744 | tf_op jit(solution)/shard_map/all_gather | solution.py:10
  59.8 1.2 slice.30
  61.0 0.0 copy-start.3
  61.0 0.0 copy-start.1
  61.0 1.2 copy.85
  62.2 0.0 all-gather.11.cloned.1.call-update
  62.2 0.0 all-gather.9.cloned.1.call-start
  62.3 1.0 slice.29
  63.2 0.9 copy.84
  64.1 0.0 all-gather.9.cloned.1.call-update
  64.1 0.0 copy-start.5
  64.1 0.0 all-gather.15.cloned.1.call-start
  64.2 2.7 fusion.42
  66.9 0.0 all-gather.15.cloned.1.call-update
  66.9 0.0 all-gather.13.cloned.1.call-start
  66.9 1.3 copy.86
  68.3 0.0 all-gather.13.cloned.1.call-update
  68.3 0.0 all-gather.17.cloned.1.call-start
  68.3 0.5 all-gather.17.cloned.1.call-update
  68.9 0.6 broadcast_in_dim.5
  69.5 5.7 %all-to-all-start = ((f32[8,1,2]{2,1,0:T(1,128)}), f32[8,1,2]{2,1,0:T(1,128)S(1)}, u32[]{:S(2)}, u32[]{:S(2)}) async-start(f32[8,1,2]{2,1,0:T(1,128)} %broadcast_in_dim.5), calls=%async_computation | async-start | bytes 8192 | tf_op jit(solution)/shard_map/all_to_all | solution.py:26
  75.2 1.4 copy.74
  76.6 0.2 convert_reduce_fusion.2
  76.8 0.3 multiply_reduce_fusion.3
  77.1 0.8 dynamic_slice.3
  77.9 2.1 all-to-all-done
  80.0 0.5 broadcast.129
  80.5 0.7 reduce.5
  81.2 0.1 mul.133
  81.3 22.1 %all-gather.11.cloned.1.call-done = bf16[1024,3,1024]{0,2,1:T(8,128)(2,1)} async-done(((bf16[1024,3,128]{0,2,1:T(8,128)(2,1)}), bf16[1024,3,1024]{0,2,1:T(8,128)(2,1)}) %all-gather.11.cloned.1.call-update) | async-done | bytes 6291472 | tf_op jit(solution)/shard_map/all_gather | solution.py:100
  103.3 8.1 %fusion.23 = f32[6,64,3,16,64]{1,4,3,2,0:T(8,128)S(1)} fusion(bf16[3,16,64,1024,1]{3,2,1,0,4:T(8,128)(2,1)} %bitcast.81, bf16[6,64,1024]{2,1,0:T(8,128)(2,1)S(1)} %copy-done.1, f32[1024]{0:T(1024)S(1)} %copy-done.5, f32[6,64]{1,0:T(8,128)S(1)} %add_rsqrt_fusion.3, f32[6,64]{1,0:T(8,128)S(1)} %broadcast_multiply_fusion.1), kind=kOutput, calls=%fused_computation.50 | convolution fusion | flops 2417885184 | bytes 11803648 | tf_op jit(solution)/shard_map/dot_general | solution.py:49
  111.4 1.2 multiply_reduce_fusion.1
  112.7 1.2 fusion.12
  113.9 2.0 fusion.19
  115.9 3.2 copy.69
  119.0 2.6 reshape_reshape.3
  121.7 8.8 %all-gather.9.cloned.1.call-done = bf16[1024,1024]{1,0:T(8,128)(2,1)} async-done(((bf16[128,1024]{1,0:T(8,128)(2,1)}), bf16[1024,1024]{1,0:T(8,128)(2,1)}) %all-gather.9.cloned.1.call-update) | async-done | bytes 2097168 | tf_op jit(solution)/shard_map/all_gather | solution.py:101
  130.5 3.5 %convert_bitcast_fusion.1 = bf16[384,8,1024]{0,2,1:T(8,128)(2,1)S(1)} fusion(bf16[8,128,1024]{2,1,0:T(8,128)(2,1)} %bitcast.76, bf16[384,8,128]{2,1,0:T(8,128)(2,1)S(1)} %reshape_reshape.3), kind=kOutput, calls=%fused_computation.20 | convolution fusion | flops 808452096 | bytes 9175040 | tf_op jit(solution)/shard_map/rgk,gkn->rgn/dot_general | solution.py:70
  134.0 0.0 copy-start.6
  134.0 2.0 convert_reduce_fusion.1
  136.0 3.0 copy.72
  139.0 1.6 fusion.33
  140.6 0.1 div.39
  140.7 1.9 multiply_reduce_fusion.2
  142.6 0.1 rsqrt.55
  142.7 39.5 %all-gather.15.cloned.1.call-done = bf16[1024,4096]{1,0:T(8,128)(2,1)} async-done(((bf16[1024,512]{1,0:T(8,128)(2,1)}), bf16[1024,4096]{1,0:T(8,128)(2,1)}) %all-gather.15.cloned.1.call-update) | async-done | bytes 8388624 | tf_op jit(solution)/shard_map/all_gather | solution.py:102
  182.2 21.2 %fusion.2 = bf16[384,4096]{1,0:T(8,128)(2,1)} fusion(bf16[1024,4096]{1,0:T(8,128)(2,1)} %all-gather.15.cloned.1.call-done, f32[384,1024]{0,1:T(8,128)} %copy.74, f32[384,1024]{0,1:T(8,128)} %convert_reduce_fusion.1, f32[1024]{0:T(1024)S(1)} %copy-done.6, f32[384]{0:T(512)S(1)} %rsqrt.55, f32[384]{0:T(512)S(1)} %div.39), kind=kOutput, calls=%fused_computation.5 | convolution fusion | flops 3325427712 | bytes 14687232 | tf_op jit(solution)/shard_map/dot_general | solution.py:111
  203.4 30.3 %all-gather.13.cloned.1.call-done = bf16[4096,1024]{1,0:T(8,128)(2,1)} async-done(((bf16[512,1024]{1,0:T(8,128)(2,1)}), bf16[4096,1024]{1,0:T(8,128)(2,1)}) %all-gather.13.cloned.1.call-update) | async-done | bytes 8388624 | tf_op jit(solution)/shard_map/all_gather | solution.py:103
  233.7 11.9 %convert_bitcast_fusion = bf16[384,8,1024]{0,2,1:T(8,128)(2,1)} fusion(bf16[8,512,1024]{2,1,0:T(8,128)(2,1)} %bitcast.80, bf16[48,8,8,512]{3,2,1,0:T(8,128)(2,1)} %bitcast.82), kind=kOutput, calls=%fused_computation.6 | convolution fusion | flops 3224371200 | bytes 17825792 | tf_op jit(solution)/shard_map/rgk,gkn->rgn/dot_general | solution.py:70
  245.6 5.1 %convert_reduce_fusion = f32[384,1024]{0,1:T(8,128)} fusion(bf16[384,8,1024]{0,2,1:T(8,128)(2,1)} %convert_bitcast_fusion), kind=kLoop, calls=%fused_computation | loop fusion | flops 5898240 | bytes 7864320 | tf_op jit(solution)/shard_map/reduce_sum | solution.py:74
  250.6 3.0 copy.77
  253.7 2.3 add_reduce_fusion
  256.0 0.1 multiply_reduce_fusion.5
  256.1 0.2 multiply_reduce_fusion.4
  256.3 0.5 multiply_reduce_fusion.6
  256.8 62.9 %all-gather.17.cloned.1.call-done = bf16[12288,768]{1,0:T(8,128)(2,1)} async-done(((bf16[96,768]{1,0:T(8,128)(2,1)}), bf16[12288,768]{1,0:T(8,128)(2,1)}) %all-gather.17.cloned.1.call-update) | async-done | bytes 18874384 | tf_op jit(solution)/shard_map/all_gather | solution.py:126
  319.7 9.0 %fusion.43 = (f32[6]{0:T(128)S(1)}, f32[6,12288]{1,0:T(8,128)S(1)}) fusion(bf16[12288,768]{1,0:T(8,128)(2,1)} %all-gather.17.cloned.1.call-done, f32[6,768]{1,0:T(8,128)S(1)} %get-tuple-element.14, f32[6]{0:T(128)S(1)} %add_rsqrt_fusion.4), kind=kOutput, calls=%fused_computation.90 | convolution fusion | flops 113329144 | bytes 19187760 | tf_op jit(solution)/shard_map/dot_general | solution.py:124
  328.8 0.3 exponential_reduce_fusion
  329.1 0.5 subtract_subtract_fusion
  (19 shorter events, 0.1 us)
Async XLA Ops:
  6.5 249.8 %copy-start = (bf16[1024,768]{1,0:T(8,128)(2,1)S(1)}, bf16[1024,768]{1,0:T(8,128)(2,1)}, u32[]{:S(2)}) copy-start(bf16[1024,768]{1,0:T(8,128)(2,1)} %param.22) | copy-start | bytes 4718596
  6.5 53.2 %all-gather.7.cloned.1.call-start = ((), (), s32[]{:S(2)}) async-start(), calls=%async_computation.1 | async-start | bytes 3342336 | tf_op jit(solution)/shard_map/all_gather | solution.py:10
  9.1 94.3 %all-gather.11.cloned.1.call-start = ((), (), s32[]{:S(2)}) async-start(), calls=%async_computation.3 | async-start | bytes 7077888 | tf_op jit(solution)/shard_map/all_gather | solution.py:100
  61.0 7.9 %copy-start.3 = (f32[2]{0:T(128)S(1)}, f32[2]{0:T(128)}, u32[]{:S(2)}) copy-start(f32[2]{0:T(128)} %param.16) | copy-start | bytes 28
  61.0 14.2 %copy-start.1 = (bf16[6,64,1024]{2,1,0:T(8,128)(2,1)S(1)}, bf16[6,64,1024]{2,1,0:T(8,128)(2,1)}, u32[]{:S(2)}) copy-start(bf16[6,64,1024]{2,1,0:T(8,128)(2,1)} %param.13) | copy-start | bytes 2359300
  62.2 68.3 %all-gather.9.cloned.1.call-start = ((), (), s32[]{:S(2)}) async-start(), calls=%async_computation.2 | async-start | bytes 2359296 | tf_op jit(solution)/shard_map/all_gather | solution.py:101
  64.1 39.2 %copy-start.5 = (f32[1024]{0:T(1024)S(1)}, f32[1024]{0:T(1024)}, u32[]{:S(2)}) copy-start(f32[1024]{0:T(1024)} %param.14) | copy-start | bytes 12292
  64.1 118.1 %all-gather.15.cloned.1.call-start = ((), (), s32[]{:S(2)}) async-start(), calls=%async_computation.5 | async-start | bytes 9437184 | tf_op jit(solution)/shard_map/all_gather | solution.py:102
  66.9 166.8 %all-gather.13.cloned.1.call-start = ((), (), s32[]{:S(2)}) async-start(), calls=%async_computation.4 | async-start | bytes 9437184 | tf_op jit(solution)/shard_map/all_gather | solution.py:103
  68.3 251.4 %all-gather.17.cloned.1.call-start = ((), (), s32[]{:S(2)}) async-start(), calls=%async_computation.6 | async-start | bytes 19021824 | tf_op jit(solution)/shard_map/all_gather | solution.py:126
  69.5 10.5 %all-to-all-start = ((f32[8,1,2]{2,1,0:T(1,128)}), f32[8,1,2]{2,1,0:T(1,128)S(1)}, u32[]{:S(2)}, u32[]{:S(2)}) async-start(f32[8,1,2]{2,1,0:T(1,128)} %broadcast_in_dim.5), calls=%async_computation | async-start | bytes 8192 | tf_op jit(solution)/shard_map/all_to_all | solution.py:26
  134.0 48.2 %copy-start.6 = (f32[1024]{0:T(1024)S(1)}, f32[1024]{0:T(1024)}, u32[]{:S(2)}) copy-start(f32[1024]{0:T(1024)} %param.18) | copy-start | bytes 12292
  245.6 10.8 %copy-start.2 = (f32[1024]{0:T(1024)S(1)}, f32[1024]{0:T(1024)}, u32[]{:S(2)}) copy-start(f32[1024]{0:T(1024)} %param.21) | copy-start | bytes 12292
  319.7 9.4 %copy-start.4 = (f32[6]{0:T(128)S(1)}, f32[6]{0:T(128)}, u32[]{:S(2)}) copy-start(f32[6]{0:T(128)} %param.25) | copy-start | bytes 76
Sparse Core Ops, SparseCore 0:
  9.5 50.2 all-gather.6
  62.3 40.9 all-gather.10
  105.0 25.4 all-gather.8
  132.0 50.1 all-gather.14
  183.8 49.8 all-gather.12
  236.6 83.0 all-gather.16
where the time goes:
time: 337 us; the launch traced here: 336 us
  waiting for transfers between devices  217 us (64%)
  matrix products  57.3 us (17%)
  local copies, waits for them, and re-layouts  24.5 us (7%)
  other arithmetic  18.1 us (5%)
  between operations  13.7 us (4%)
  starting transfers between devices  5.93 us (2%)
    all_gather x1, waiting for transfers between devices, shards(): lax.all_gather(text_bank, ('dp', 'mp'), axis=0, tiled=True)  62.9 us
    all_gather x1, waiting for transfers between devices, gather_turned(): result, at, outs = (lax.all_gather(both, axis, axis=0, tiled=True), 0, [])  50.7 us
    all_gather x1, waiting for transfers between devices, shards(): lax.all_gather(up_full, 'mp', axis=1, tiled=True)  39.5 us
    all_gather x1, waiting for transfers between devices, shards(): lax.all_gather(down_full, 'mp', axis=0, tiled=True)  30.3 us
    all_gather x1, waiting for transfers between devices, shards(): lax.all_gather(joint_full, 'mp', axis=2, tiled=True)  22.1 us
    dot_general x1, matrix products, shards(): upper = jnp.dot(normed_second, up_all, preferred_element_type=jnp.float32)  21.2 us
    dot_general x2, matrix products, grouped_local(): jnp.einsum('rgk,gkn->rgn', left_groups, right_groups, preferred_element_t...  15.4 us
    dot_general x1, matrix products, shards(): lax.dot_general(image_units, lax.all_gather(text_bank, ('dp', 'mp'), axis...  9.03 us
  transfers between devices with their start and end apart: 7, of which 7 were waited for; matrix products, arithmetic and copies ran while one was open for 25% of the time, Pallas kernels for 0%

commit v1 on v0

--- a/solution.py
+++ b/solution.py
@@ -97,7 +97,7 @@
     normed_first = layer_norm(residual, gain_first).astype(jnp.bfloat16)
     groups = lax.axis_size("mp")
     joint_all, output_all, up_all, down_all = (
-        lax.all_gather(joint_full, "mp", axis=2, tiled=True),
+        jnp.concatenate(lax.all_gather(joint_full, "mp"), axis=2),
         lax.all_gather(output_full, "mp", axis=0, tiled=True),
         lax.all_gather(up_full, "mp", axis=1, tiled=True),
         lax.all_gather(down_full, "mp", axis=0, tiled=True),

time: 337 us -> 338 us (level)
  waiting for transfers between devices: 217 us -> 208 us
  local copies, waits for them, and re-layouts: 24.5 us -> 33.4 us
    all_gather x1, waiting for transfers between devices: 8.83 us -> 0.17 us  [shards(): lax.all_gather(output_full, 'mp', axis=0, tiled=True)]
    all_gather x0 -> x1, local copies, waits for them, and re-layouts: none -> 8.63 us  [shards(): lax.all_gather(joint_full, 'mp')]
  transfers between devices with their start and end apart: 7 -> 7, of which waited for: 7 -> 7; matrix products, arithmetic and copies ran while one was open for 25% -> 28% of each run, Pallas kernels for 0% -> 0%
where the time goes in v1:
time: 338 us; the launch traced here: 337 us
  waiting for transfers between devices  208 us (62%)
  matrix products  57.4 us (17%)
  local copies, waits for them, and re-layouts  33.4 us (10%)
  other arithmetic  18.2 us (5%)
  between operations  13.7 us (4%)
  starting transfers between devices  5.93 us (2%)
    all_gather x1, waiting for transfers between devices, shards(): lax.all_gather(text_bank, ('dp', 'mp'), axis=0, tiled=True)  62.9 us
    all_gather x1, waiting for transfers between devices, gather_turned(): result, at, outs = (lax.all_gather(both, axis, axis=0, tiled=True), 0, [])  50.7 us
    all_gather x1, waiting for transfers between devices, shards(): lax.all_gather(up_full, 'mp', axis=1, tiled=True)  39.5 us
    all_gather x1, waiting for transfers between devices, shards(): lax.all_gather(down_full, 'mp', axis=0, tiled=True)  30.3 us
    all_gather x1, waiting for transfers between devices, shards(): lax.all_gather(joint_full, 'mp')  22.2 us
    dot_general x1, matrix products, shards(): upper = jnp.dot(normed_second, up_all, preferred_element_type=jnp.float32)  21.2 us
    dot_general x2, matrix products, grouped_local(): jnp.einsum('rgk,gkn->rgn', left_groups, right_groups, preferred_element_t...  15.4 us
    dot_general x1, matrix products, shards(): lax.dot_general(image_units, lax.all_gather(text_bank, ('dp', 'mp'), axis...  9.03 us
  transfers between devices with their start and end apart: 7, of which 7 were waited for; matrix products, arithmetic and copies ran while one was open for 28% of the time, Pallas kernels for 0%

profile of v1, /device:TPU:1, one launch (start us, length us, event | category | flops | bytes accessed | tf_op | source)
XLA Modules:
  0.0 336.8 jit_solution(6643877292453016603)
XLA Ops:
  6.5 0.9 copy_bitcast_fusion
  7.5 1.6 pad_maximum_fusion
  9.0 0.0 all-gather.7.cloned.1.call-update
  9.1 0.0 all-gather.11.cloned.1.call-start
  9.1 50.7 %all-gather.7.cloned.1.call-done = bf16[1024,1536]{1,0:T(8,128)(2,1)} async-done(((bf16[64,1536]{1,0:T(8,128)(2,1)}), bf16[1024,1536]{1,0:T(8,128)(2,1)}) %all-gather.7.cloned.1.call-update) | async-done | bytes 3145744 | tf_op jit(solution)/shard_map/all_gather | solution.py:10
  59.8 1.2 slice.30
  61.0 0.3 copy.105
  61.3 0.0 copy-start.3
  61.3 0.0 copy-start.1
  61.3 1.2 copy.84
  62.5 0.0 all-gather.11.cloned.1.call-update
  62.5 0.0 all-gather.9.cloned.1.call-start
  62.6 1.0 slice.29
  63.5 0.9 copy.104
  64.4 0.0 all-gather.9.cloned.1.call-update
  64.4 0.0 all-gather.15.cloned.1.call-start
  64.5 2.7 fusion.42
  67.1 0.0 all-gather.15.cloned.1.call-update
  67.2 0.0 all-gather.13.cloned.1.call-start
  67.2 1.3 copy.106
  68.5 0.0 all-gather.13.cloned.1.call-update
  68.6 0.0 all-gather.17.cloned.1.call-start
  68.6 0.5 all-gather.17.cloned.1.call-update
  69.2 0.6 broadcast_in_dim.5
  69.7 5.7 %all-to-all-start = ((f32[8,1,2]{2,1,0:T(1,128)}), f32[8,1,2]{2,1,0:T(1,128)S(1)}, u32[]{:S(2)}, u32[]{:S(2)}) async-start(f32[8,1,2]{2,1,0:T(1,128)} %broadcast_in_dim.5), calls=%async_computation | async-start | bytes 8192 | tf_op jit(solution)/shard_map/all_to_all | solution.py:26
  75.5 1.4 copy.94
  76.9 0.2 convert_reduce_fusion.2
  77.1 0.3 multiply_reduce_fusion.3
  77.4 0.8 dynamic_slice.3
  78.2 2.0 all-to-all-done
  80.2 0.5 broadcast.129
  80.7 0.7 reduce.5
  81.3 0.1 mul.133
  81.4 22.2 %all-gather.11.cloned.1.call-done = bf16[8,1024,3,128]{3,1,2,0:T(8,128)(2,1)} async-done(((bf16[1,1024,3,128]{3,1,2,0:T(8,128)(2,1)}), bf16[8,1024,3,128]{3,1,2,0:T(8,128)(2,1)}) %all-gather.11.cloned.1.call-update) | async-done | bytes 6291472 | tf_op jit(solution)/shard_map/all_gather | solution.py:100
  103.6 8.6 %copy.85 = bf16[8,1024,3,128]{1,3,0,2:T(8,128)(2,1)} copy(bf16[8,1024,3,128]{3,1,2,0:T(8,128)(2,1)} %all-gather.11.cloned.1.call-done) | data formatting | bytes 12582912 | tf_op jit(solution)/shard_map/all_gather | solution.py:100
  112.2 8.2 %fusion.23 = f32[6,64,3,16,64]{1,4,3,2,0:T(8,128)S(1)} fusion(bf16[3,16,64,1024,1]{3,2,1,0,4:T(8,128)(2,1)} %bitcast.75, bf16[6,64,1024]{2,1,0:T(8,128)(2,1)S(1)} %copy-done.1, f32[1024]{0:T(1024)S(1)} %copy-done.5, f32[6,64]{1,0:T(8,128)S(1)} %add_rsqrt_fusion.3, f32[6,64]{1,0:T(8,128)S(1)} %broadcast_multiply_fusion.1), kind=kOutput, calls=%fused_computation.50 | convolution fusion | flops 2417885184 | bytes 11803648 | tf_op jit(solution)/shard_map/dot_general | solution.py:49
  120.4 1.2 multiply_reduce_fusion.1
  121.7 1.2 fusion.12
  122.8 2.0 fusion.19
  124.8 3.2 copy.89
  128.0 2.6 reshape_reshape.7
  130.6 0.2 all-gather.9.cloned.1.call-done
  130.8 3.5 %convert_bitcast_fusion.1 = bf16[384,8,1024]{0,2,1:T(8,128)(2,1)S(1)} fusion(bf16[8,128,1024]{2,1,0:T(8,128)(2,1)} %bitcast.79, bf16[384,8,128]{2,1,0:T(8,128)(2,1)S(1)} %reshape_reshape.7), kind=kOutput, calls=%fused_computation.20 | convolution fusion | flops 808452096 | bytes 9175040 | tf_op jit(solution)/shard_map/rgk,gkn->rgn/dot_general | solution.py:70
  134.3 0.0 copy-start.6
  134.3 2.0 convert_reduce_fusion.1
  136.3 3.0 copy.92
  139.3 1.6 fusion.33
  140.9 0.1 div.39
  141.0 1.9 multiply_reduce_fusion.2
  142.9 0.1 rsqrt.55
  143.0 39.5 %all-gather.15.cloned.1.call-done = bf16[1024,4096]{1,0:T(8,128)(2,1)} async-done(((bf16[1024,512]{1,0:T(8,128)(2,1)}), bf16[1024,4096]{1,0:T(8,128)(2,1)}) %all-gather.15.cloned.1.call-update) | async-done | bytes 8388624 | tf_op jit(solution)/shard_map/all_gather | solution.py:102
  182.5 21.2 %fusion.2 = bf16[384,4096]{1,0:T(8,128)(2,1)} fusion(bf16[1024,4096]{1,0:T(8,128)(2,1)} %all-gather.15.cloned.1.call-done, f32[384,1024]{0,1:T(8,128)} %copy.94, f32[384,1024]{0,1:T(8,128)} %convert_reduce_fusion.1, f32[1024]{0:T(1024)S(1)} %copy-done.6, f32[384]{0:T(512)S(1)} %rsqrt.55, f32[384]{0:T(512)S(1)} %div.39), kind=kOutput, calls=%fused_computation.5 | convolution fusion | flops 3325427712 | bytes 14687232 | tf_op jit(solution)/shard_map/dot_general | solution.py:111
  203.7 30.3 %all-gather.13.cloned.1.call-done = bf16[4096,1024]{1,0:T(8,128)(2,1)} async-done(((bf16[512,1024]{1,0:T(8,128)(2,1)}), bf16[4096,1024]{1,0:T(8,128)(2,1)}) %all-gather.13.cloned.1.call-update) | async-done | bytes 8388624 | tf_op jit(solution)/shard_map/all_gather | solution.py:103
  234.0 11.9 %convert_bitcast_fusion = bf16[384,8,1024]{0,2,1:T(8,128)(2,1)} fusion(bf16[8,512,1024]{2,1,0:T(8,128)(2,1)} %bitcast.83, bf16[48,8,8,512]{3,2,1,0:T(8,128)(2,1)} %bitcast.84), kind=kOutput, calls=%fused_computation.6 | convolution fusion | flops 3224371200 | bytes 17825792 | tf_op jit(solution)/shard_map/rgk,gkn->rgn/dot_general | solution.py:70
  245.9 5.1 %convert_reduce_fusion = f32[384,1024]{0,1:T(8,128)} fusion(bf16[384,8,1024]{0,2,1:T(8,128)(2,1)} %convert_bitcast_fusion), kind=kLoop, calls=%fused_computation | loop fusion | flops 5898240 | bytes 7864320 | tf_op jit(solution)/shard_map/reduce_sum | solution.py:74
  250.9 3.0 copy.97
  253.9 2.3 add_reduce_fusion
  256.3 0.1 multiply_reduce_fusion.5
  256.4 0.2 multiply_reduce_fusion.4
  256.6 0.5 multiply_reduce_fusion.6
  257.1 62.9 %all-gather.17.cloned.1.call-done = bf16[12288,768]{1,0:T(8,128)(2,1)} async-done(((bf16[96,768]{1,0:T(8,128)(2,1)}), bf16[12288,768]{1,0:T(8,128)(2,1)}) %all-gather.17.cloned.1.call-update) | async-done | bytes 18874384 | tf_op jit(solution)/shard_map/all_gather | solution.py:126
  320.0 9.0 %fusion.43 = (f32[6]{0:T(128)S(1)}, f32[6,12288]{1,0:T(8,128)S(1)}) fusion(bf16[12288,768]{1,0:T(8,128)(2,1)} %all-gather.17.cloned.1.call-done, f32[6,768]{1,0:T(8,128)S(1)} %get-tuple-element.14, f32[6]{0:T(128)S(1)} %add_rsqrt_fusion.4), kind=kOutput, calls=%fused_computation.90 | convolution fusion | flops 113329144 | bytes 19187760 | tf_op jit(solution)/shard_map/dot_general | solution.py:124
  329.1 0.3 exponential_reduce_fusion
  329.4 0.5 subtract_subtract_fusion
  (21 shorter events, 0.1 us)
Async XLA Ops:
  6.5 250.1 %copy-start = (bf16[1024,768]{1,0:T(8,128)(2,1)S(1)}, bf16[1024,768]{1,0:T(8,128)(2,1)}, u32[]{:S(2)}) copy-start(bf16[1024,768]{1,0:T(8,128)(2,1)} %param.22) | copy-start | bytes 4718596
  6.5 53.2 %all-gather.7.cloned.1.call-start = ((), (), s32[]{:S(2)}) async-start(), calls=%async_computation.1 | async-start | bytes 3342336 | tf_op jit(solution)/shard_map/all_gather | solution.py:10
  9.1 94.5 %all-gather.11.cloned.1.call-start = ((), (), s32[]{:S(2)}) async-start(), calls=%async_computation.3 | async-start | bytes 7077888 | tf_op jit(solution)/shard_map/all_gather | solution.py:100
  61.3 7.9 %copy-start.3 = (f32[2]{0:T(128)S(1)}, f32[2]{0:T(128)}, u32[]{:S(2)}) copy-start(f32[2]{0:T(128)} %param.16) | copy-start | bytes 28
  61.3 14.2 %copy-start.1 = (bf16[6,64,1024]{2,1,0:T(8,128)(2,1)S(1)}, bf16[6,64,1024]{2,1,0:T(8,128)(2,1)}, u32[]{:S(2)}) copy-start(bf16[6,64,1024]{2,1,0:T(8,128)(2,1)} %param.13) | copy-start | bytes 2359300
  62.5 68.3 %all-gather.9.cloned.1.call-start = ((), (), s32[]{:S(2)}) async-start(), calls=%async_computation.2 | async-start | bytes 2359296 | tf_op jit(solution)/shard_map/all_gather | solution.py:101
  64.4 118.1 %all-gather.15.cloned.1.call-start = ((), (), s32[]{:S(2)}) async-start(), calls=%async_computation.5 | async-start | bytes 9437184 | tf_op jit(solution)/shard_map/all_gather | solution.py:102
  67.2 166.8 %all-gather.13.cloned.1.call-start = ((), (), s32[]{:S(2)}) async-start(), calls=%async_computation.4 | async-start | bytes 9437184 | tf_op jit(solution)/shard_map/all_gather | solution.py:103
  68.6 251.4 %all-gather.17.cloned.1.call-start = ((), (), s32[]{:S(2)}) async-start(), calls=%async_computation.6 | async-start | bytes 19021824 | tf_op jit(solution)/shard_map/all_gather | solution.py:126
  69.7 10.4 %all-to-all-start = ((f32[8,1,2]{2,1,0:T(1,128)}), f32[8,1,2]{2,1,0:T(1,128)S(1)}, u32[]{:S(2)}, u32[]{:S(2)}) async-start(f32[8,1,2]{2,1,0:T(1,128)} %broadcast_in_dim.5), calls=%async_computation | async-start | bytes 8192 | tf_op jit(solution)/shard_map/all_to_all | solution.py:26
  81.4 30.8 %copy-start.5 = (f32[1024]{0:T(1024)S(1)}, f32[1024]{0:T(1024)}, u32[]{:S(2)}) copy-start(f32[1024]{0:T(1024)} %param.14) | copy-start | bytes 12292
  134.3 48.2 %copy-start.6 = (f32[1024]{0:T(1024)S(1)}, f32[1024]{0:T(1024)}, u32[]{:S(2)}) copy-start(f32[1024]{0:T(1024)} %param.18) | copy-start | bytes 12292
  245.9 10.8 %copy-start.2 = (f32[1024]{0:T(1024)S(1)}, f32[1024]{0:T(1024)}, u32[]{:S(2)}) copy-start(f32[1024]{0:T(1024)} %param.21) | copy-start | bytes 12292
  320.0 9.4 %copy-start.4 = (f32[6]{0:T(128)S(1)}, f32[6]{0:T(128)}, u32[]{:S(2)}) copy-start(f32[6]{0:T(128)} %param.25) | copy-start | bytes 76
Sparse Core Ops, SparseCore 0:
  9.5 50.2 all-gather.6
  62.6 40.9 all-gather.10
  105.3 25.4 all-gather.8
  132.3 50.1 all-gather.14
  184.0 49.8 all-gather.12
  236.9 83.1 all-gather.16
